TPU v7x, 32 devices: a whole 2x2x4 slice. The times are simulated.
32 devices in a mesh: ea: 8 (over z, y), sa: 4 (over x, core).
Axes of the slice: x: 2, y: 2, z: 4, core: 2. Of those that a mesh axis runs over, the one named last changes fastest.
Arguments:
- lesser: bfloat16 [2, 1024, 2, 256, 256], P(None, 'ea', None, 'sa'), may hold values from -30 to 30, as said below
- greater: bfloat16 [2, 1024, 2, 256, 256], P(None, 'ea', None, 'sa'), may hold values from -30 to 30, as said below
Outputs:
- polar: float32 [2, 1024, 2, 256, 256], P(None, 'ea', None, 'sa')
- pol_norm: float32 [1], replicated
Inputs may be any that keep to these rules, and one draw needn't show every extreme that they name: `lesser`: Real-valued entries, independent from energy to energy. `greater`: Real-valued entries, independent from energy to energy.
All inputs are finite; a program needn't handle non-finite values.
Results may differ from a plain program's by a relative error of at most 0.0049.
Values may be sent and summed in bfloat16 or wider, within the bound.
A program may use at most 320 MiB of HBM per device.

v0:
```python
import math

import jax
import jax.numpy as jnp
from jax import lax
from jax.sharding import PartitionSpec as P

NE = 1024
ORB = 256
BLOCKS = 2


def energy_tables(count):
    index = jnp.arange(count, dtype=jnp.int32)
    phase = index[:, None] * index[None, :] % count
    angle = phase.astype(jnp.float32) * (2.0 * math.pi / count)
    return (jnp.cos(angle).astype(jnp.bfloat16), jnp.sin(angle).astype(jnp.bfloat16))


def spectra(columns, cosine, sine):
    stacked = jnp.concatenate(columns, axis=1)
    return (
        jnp.dot(cosine, stacked, preferred_element_type=jnp.float32),
        jnp.dot(sine, stacked, preferred_element_type=jnp.float32),
    )


def split_spectrum(cos_part, sin_part, which, width):
    real_cols = slice(2 * which * width, (2 * which + 1) * width)
    imag_cols = slice((2 * which + 1) * width, (2 * which + 2) * width)
    spec_re = cos_part[:, real_cols] + sin_part[:, imag_cols]
    spec_im = cos_part[:, imag_cols] - sin_part[:, real_cols]
    return (spec_re, spec_im)


def polarize(less_re, less_im, great_re, great_im, cosine, sine, count):
    width = less_re.shape[1]
    prod_re = (less_re * great_re + less_im * great_im).astype(jnp.bfloat16)
    prod_im = (less_im * great_re - less_re * great_im).astype(jnp.bfloat16)
    cos_part, sin_part = spectra([prod_re, prod_im], cosine, sine)
    corr_re = cos_part[:, :width] - sin_part[:, width:]
    corr_im = cos_part[:, width:] + sin_part[:, :width]
    weight = float(count) ** (-1.5)
    return jnp.stack([weight * corr_im, -weight * corr_re])


def both_spectra(less_pairs, great_pairs, cosine, sine):
    energies = less_pairs.shape[1]
    width = less_pairs[0].size // energies
    cos_part, sin_part = spectra(
        [
            less_pairs[0].reshape(energies, width),
            less_pairs[1].reshape(energies, width),
            great_pairs[0].reshape(energies, width),
            great_pairs[1].reshape(energies, width),
        ],
        cosine,
        sine,
    )
    less_re, less_im = split_spectrum(cos_part, sin_part, 0, width)
    great_re, great_im = split_spectrum(cos_part, sin_part, 1, width)
    return (less_re, less_im, great_re, great_im)


def body(lesser, greater):
    cosine, sine = energy_tables(NE)
    less_pairs, great_pairs = (
        lax.all_to_all(lesser, "ea", split_axis=4, concat_axis=1, tiled=True),
        lax.all_to_all(greater, "ea", split_axis=4, concat_axis=1, tiled=True),
    )
    shape = less_pairs.shape
    less_re, less_im, great_re, great_im = both_spectra(less_pairs, great_pairs, cosine, sine)
    polar_local = polarize(less_re, less_im, great_re, great_im, cosine, sine, NE).reshape(shape)
    total = jnp.sum(polar_local * polar_local)
    polar = lax.all_to_all(polar_local, "ea", split_axis=1, concat_axis=4, tiled=True)
    norm_total = lax.psum(total, ("ea", "sa"))
    pol_norm = jnp.sqrt(norm_total / (NE * BLOCKS * ORB * ORB) + 1e-06).reshape(1)
    return (polar, pol_norm)


def solution(mesh):
    return jax.shard_map(
        body,
        mesh=mesh,
        in_specs=(P(None, "ea", None, "sa", None), P(None, "ea", None, "sa", None)),
        out_specs=(P(None, "ea", None, "sa", None), P()),
        check_vma=False,
    )
```

profile of v0, /device:TPU:0, one launch (start us, length us, event | category | flops | bytes accessed | tf_op | source)
XLA Modules:
  0.0 2305.2 jit_solution(13442088749279677112)
XLA Ops:
  0.6 25.8 %copy.41 = bf16[2,128,2,64,256]{1,3,2,0,4:T(8,128)(2,1)} copy(bf16[2,128,2,64,256]{4,3,2,1,0:T(8,128)(2,1)} %param.2) | data formatting | bytes 33554432 | tf_op args[0]
  33.7 25.9 %copy.45 = bf16[2,128,2,64,256]{1,3,2,0,4:T(8,128)(2,1)} copy(bf16[2,128,2,64,256]{4,3,2,1,0:T(8,128)(2,1)} %param.3) | data formatting | bytes 33554432 | tf_op args[1]
  59.7 337.0 %all-to-all-done = bf16[2,128,2,64,256]{1,3,2,0,4:T(8,128)(2,1)} async-done(((bf16[2,128,2,64,256]{1,3,2,0,4:T(8,128)(2,1)}), bf16[2,128,2,64,256]{1,3,2,0,4:T(8,128)(2,1)}, u32[]{:S(2)}, u32[]{:S(2)}) %all-to-all-start) | async-done | bytes 16777248 | tf_op jit(solution)/shard_map/all_to_all | solution.py:68
  402.5 16.3 cosine_convert_fusion.9
  418.7 15.7 sine_convert_fusion.9
  434.4 16.3 cosine_convert_fusion.8
  450.7 16.4 sine_convert_fusion.8
  526.4 238.1 %all-to-all-done.1 = bf16[2,128,2,64,256]{1,3,2,0,4:T(8,128)(2,1)} async-done(((bf16[2,128,2,64,256]{1,3,2,0,4:T(8,128)(2,1)}), bf16[2,128,2,64,256]{1,3,2,0,4:T(8,128)(2,1)}, u32[]{:S(2)}, u32[]{:S(2)}) %all-to-all-start.1) | async-done | bytes 16777248 | tf_op jit(solution)/shard_map/all_to_all | solution.py:69
  842.7 45.0 %fusion.10 = f32[1024,16384]{1,0:T(8,128)} fusion(bf16[1024,16384]{0,1:T(8,128)(2,1)} %bitcast_dynamic-update-slice_fusion, bf16[1024,1024]{1,0:T(8,128)(2,1)} %cosine_convert_fusion.9), kind=kOutput, calls=%fused_computation.30 | convolution fusion | flops 34359738368 | bytes 102760448 | tf_op jit(solution)/shard_map/dot_general | solution.py:23
  887.7 44.3 %fusion.11 = f32[1024,16384]{1,0:T(8,128)} fusion(bf16[1024,16384]{0,1:T(8,128)(2,1)} %bitcast_dynamic-update-slice_fusion, bf16[1024,1024]{1,0:T(8,128)(2,1)S(1)} %sine_convert_fusion.9), kind=kOutput, calls=%fused_computation.31 | convolution fusion | flops 34359738368 | bytes 102760448 | tf_op jit(solution)/shard_map/dot_general | solution.py:24
  931.9 49.1 %add_convert_fusion = (bf16[1024,4096]{1,0:T(8,128)(2,1)}, bf16[1024,4096]{1,0:T(8,128)(2,1)}) fusion(f32[1024,16384]{1,0:T(8,128)} %fusion.11, f32[1024,16384]{1,0:T(8,128)} %fusion.10), kind=kLoop, calls=%fused_computation.12 | loop fusion | flops 50331648 | bytes 150994944 | tf_op jit(solution)/shard_map/convert_element_type | solution.py:38
  981.0 26.1 %fusion.3 = f32[1024,8192]{1,0:T(8,128)} fusion(bf16[1024,4096]{1,0:T(8,128)(2,1)} %get-tuple-element.11, bf16[1024,4096]{1,0:T(8,128)(2,1)} %get-tuple-element.10, bf16[1024,1024]{1,0:T(8,128)(2,1)} %cosine_convert_fusion.8), kind=kOutput, calls=%fused_computation.14 | convolution fusion | flops 17213423616 | bytes 52428800 | tf_op jit(solution)/shard_map/dot_general | solution.py:23
  1007.1 25.7 %fusion.2 = f32[1024,8192]{1,0:T(8,128)} fusion(bf16[1024,4096]{1,0:T(8,128)(2,1)} %get-tuple-element.11, bf16[1024,4096]{1,0:T(8,128)(2,1)} %get-tuple-element.10, bf16[1024,1024]{1,0:T(8,128)(2,1)S(1)} %copy-done), kind=kOutput, calls=%fused_computation.13 | convolution fusion | flops 17213423616 | bytes 52428800 | tf_op jit(solution)/shard_map/dot_general | solution.py:24
  1032.9 34.7 %fusion.1 = (f32[1024,4096]{1,0:T(8,128)}, f32[1024,4096]{1,0:T(8,128)}) fusion(f32[1024,8192]{1,0:T(8,128)} %fusion.2, f32[1024,8192]{1,0:T(8,128)} %fusion.3), kind=kLoop, calls=%fused_computation.5 | loop fusion | flops 16777216 | bytes 100663296 | tf_op jit(solution)/shard_map/mul | solution.py:44
  1067.5 17.4 copy.49
  1085.0 17.5 copy.50
  1102.5 26.3 %multiply_reduce_fusion = (f32[]{:T(128)}, f32[2,1024,2,64,32]{1,4,3,2,0:T(8,128)}) fusion(f32[1,1024,2,64,32]{1,4,3,2,0:T(8,128)} %bitcast.50, f32[1,1024,2,64,32]{1,4,3,2,0:T(8,128)} %bitcast.49), kind=kLoop, calls=%fused_computation.1 | loop fusion | flops 25165824 | bytes 67108864 | tf_op jit(solution)/shard_map/reduce_sum | solution.py:74
  1128.7 59.1 %copy.51 = f32[2,1024,2,64,32]{3,4,2,0,1:T(8,128)} copy(f32[2,1024,2,64,32]{1,4,3,2,0:T(8,128)} %get-tuple-element.15) | data formatting | bytes 67108864 | tf_op jit(solution)/shard_map/stack | solution.py:44
  1187.8 84.9 %reshape.21 = f32[8,1,1048576]{2,1,0:T(1,128)} reshape(f32[1024,2,2,32,64]{4,3,2,1,0:T(8,128)} %bitcast.38) | data formatting | bytes 67108864
  1279.8 741.6 %psum.7 = f32[]{:T(128)} all-reduce(f32[]{:T(128)} %get-tuple-element.14), channel_id=1, replica_groups=mesh['ea'=8,'sa'=4] {'ea','sa'}, use_global_device_ids=true, to_apply=%region_1.2 | all-reduce | flops 1 | bytes 8 | tf_op jit(solution)/shard_map/psum | solution.py:76
  2022.7 98.8 %reduce = f32[8,1048576]{1,0:T(8,128)} reduce(f32[8,1,1048576]{2,1,0:T(1,128)} %all-to-all-done.2, f32[]{:T(128)} %broadcast.30), dimensions={1}, to_apply=%all_to_all.41.reduce_sub_computation | reduce | bytes 67108864 | tf_op jit(solution)/shard_map/all_to_all | solution.py:75
  2121.5 91.3 %reshape.22 = f32[1024,2,2,32,64]{4,3,2,1,0:T(8,128)} reshape(f32[8,1048576]{1,0:T(8,128)} %reduce) | data formatting | bytes 67108864
  2212.8 56.9 %copy.53 = f32[2,128,2,64,8,32]{1,5,4,3,2,0:T(8,128)} copy(f32[2,128,2,64,8,32]{3,5,2,0,1,4:T(8,128)} %bitcast.10) | data formatting | bytes 67108864 | tf_op jit(solution)/shard_map/all_to_all | solution.py:75
  2269.8 33.8 %copy.54 = f32[2,128,2,64,256]{4,3,2,1,0:T(8,128)} copy(f32[2,128,2,64,256]{1,4,3,2,0:T(8,128)} %bitcast.48) | data formatting | bytes 67108864
  (19 shorter events, 158.1 us)
Async XLA Ops:
  26.4 370.3 %all-to-all-start = ((bf16[2,128,2,64,256]{1,3,2,0,4:T(8,128)(2,1)}), bf16[2,128,2,64,256]{1,3,2,0,4:T(8,128)(2,1)}, u32[]{:S(2)}, u32[]{:S(2)}) async-start(bf16[2,128,2,64,256]{1,3,2,0,4:T(8,128)(2,1)} %copy.41), calls=%async_computation | async-start | bytes 33554432 | tf_op jit(solution)/shard_map/all_to_all | solution.py:68
  396.7 367.8 %all-to-all-start.1 = ((bf16[2,128,2,64,256]{1,3,2,0,4:T(8,128)(2,1)}), bf16[2,128,2,64,256]{1,3,2,0,4:T(8,128)(2,1)}, u32[]{:S(2)}, u32[]{:S(2)}) async-start(bf16[2,128,2,64,256]{1,3,2,0,4:T(8,128)(2,1)} %copy.45), calls=%async_computation.1 | async-start | bytes 33554432 | tf_op jit(solution)/shard_map/all_to_all | solution.py:69
  981.0 26.1 %copy-start = (bf16[1024,1024]{1,0:T(8,128)(2,1)S(1)}, bf16[1024,1024]{1,0:T(8,128)(2,1)}, u32[]{:S(2)}) copy-start(bf16[1024,1024]{1,0:T(8,128)(2,1)} %sine_convert_fusion.8) | copy-start | bytes 6291460
  1272.8 749.4 %all-to-all-start.2 = ((f32[8,1,1048576]{2,1,0:T(1,128)}), f32[8,1,1048576]{2,1,0:T(1,128)}, u32[]{:S(2)}, u32[]{:S(2)}) async-start(f32[8,1,1048576]{2,1,0:T(1,128)} %reshape.21), calls=%async_computation.2 | async-start | bytes 67108864 | tf_op jit(solution)/shard_map/all_to_all | solution.py:75
where the time goes:
time: 2320 us; the launch traced here: 2310 us
  blocking collectives  742 us (32%)
  waiting for transfers between devices  575 us (25%)
  local copies, waits for them, and re-layouts  551 us (24%)
  other arithmetic  273 us (12%)
  matrix products  141 us (6%)
    psum x1, blocking collectives, body(): norm_total = lax.psum(total, ('ea', 'sa'))  742 us
    all_to_all x1, waiting for transfers between devices, body(): lax.all_to_all(lesser, 'ea', split_axis=4, concat_axis=1, tiled=True)  337 us
    unnamed x10, local copies, waits for them, and re-layouts  290 us
    all_to_all x1, waiting for transfers between devices, body(): lax.all_to_all(greater, 'ea', split_axis=4, concat_axis=1, tiled=True)  238 us
    all_to_all x1, other arithmetic, body(): lax.all_to_all(polar_local, 'ea', split_axis=1, concat_axis=4, tiled=True)  98.8 us
    dot_general x2, matrix products, spectra(): jnp.dot(cosine, stacked, preferred_element_type=jnp.float32)  71.1 us
    dot_general x2, matrix products, spectra(): jnp.dot(sine, stacked, preferred_element_type=jnp.float32)  70 us
    another operation x1, local copies, waits for them, and re-layouts, polarize(): return jnp.stack([weight * corr_im, -weight * corr_re])  59.1 us
  transfers between devices with their start and end apart: 3, of which 2 were waited for; matrix products, arithmetic and copies ran while one was open for 6% of the time, Pallas kernels for 0%

commit v1 on v0

v1 whole, which is shorter than its diff:
```python
import functools
import math

import jax
import jax.numpy as jnp
from jax import lax
from jax.experimental import pallas as pl
from jax.experimental.pallas import tpu as pltpu
from jax.sharding import PartitionSpec as P

LANES = 128


def energy_tables(count):
    index = jnp.arange(count, dtype=jnp.int32)
    phase = index[:, None] * index[None, :] % count
    angle = phase.astype(jnp.float32) * (2.0 * math.pi / count)
    return (jnp.cos(angle).astype(jnp.bfloat16), jnp.sin(angle).astype(jnp.bfloat16))


def pack_kernel(peers, per, less_ref, great_ref, *rest):
    target, wide = rest[-2:]
    for index, source in enumerate((less_ref, great_ref)):
        for part in range(2):
            wide[...] = source[part, :, 0].astype(jnp.float32)
            field = 2 * index + part
            for peer in range(peers):
                for row in range(per):
                    at = (4 * row + field) * LANES
                    target[peer, :, at : at + LANES] = wide[
                        :, peer * per + row, :
                    ].astype(jnp.bfloat16)


def pack(lesser, greater, block, half, peers, after):
    _, energies, _, rows, _ = lesser.shape
    per = rows // peers
    width = per * 4 * LANES
    step = min(32, energies)
    source = pl.BlockSpec((2, step, 1, rows, LANES), lambda e: (0, e, block, 0, half))
    out = jax.ShapeDtypeStruct((peers, energies, width), jnp.bfloat16)
    return pl.pallas_call(
        functools.partial(pack_kernel, peers, per),
        grid=(energies // step,),
        out_shape=out,
        in_specs=[source, source]
        + [pl.BlockSpec(memory_space=pl.ANY) for _ in after],
        out_specs=pl.BlockSpec((peers, step, width), lambda e: (0, e, 0)),
        scratch_shapes=[pltpu.VMEM((step, rows, LANES), jnp.float32)],
        cost_estimate=pl.CostEstimate(
            flops=0, bytes_accessed=4 * out.size, transcendentals=0
        ),
        name="pack",
    )(lesser, greater, *after)


def unpack_kernel(peers, per, source, *rest):
    target = rest[-1]
    for part in range(2):
        for peer in range(peers):
            for row in range(per):
                at = (2 * row + part) * LANES
                target[part, :, 0, peer * per + row, :] = source[
                    peer, :, at : at + LANES
                ].astype(jnp.float32)


def unpack(arrived, polar, block, half, shape):
    peers, energies, width = arrived.shape
    rows = shape[3]
    per = rows // peers
    step = min(32, energies)
    extra = [] if polar is None else [polar]
    return pl.pallas_call(
        functools.partial(unpack_kernel, peers, per),
        grid=(energies // step,),
        out_shape=jax.ShapeDtypeStruct(shape, jnp.float32),
        in_specs=[pl.BlockSpec((peers, step, width), lambda e: (0, e, 0))]
        + [pl.BlockSpec(memory_space=pl.ANY) for _ in extra],
        out_specs=pl.BlockSpec(
            (2, step, 1, rows, LANES), lambda e: (0, e, block, 0, half)
        ),
        input_output_aliases={1: 0} if extra else {},
        cost_estimate=pl.CostEstimate(
            flops=0, bytes_accessed=6 * arrived.size, transcendentals=0
        ),
        name="unpack",
    )(arrived, *extra)


def correlate_kernel(tile, weight, cosine, sine, columns, sent, total, prod):
    w = LANES
    count = cosine.shape[0]

    @pl.when(pl.program_id(0) == 0)
    def _():
        total[...] = jnp.zeros_like(total)

    @pl.loop(0, count // tile)
    def _(k):
        rows = pl.ds(pl.multiple_of(k * tile, tile), tile)
        c = jnp.dot(cosine[rows, :], columns[...], preferred_element_type=jnp.float32)
        s = jnp.dot(sine[rows, :], columns[...], preferred_element_type=jnp.float32)
        less_re = c[:, :w] + s[:, w : 2 * w]
        less_im = c[:, w : 2 * w] - s[:, :w]
        great_re = c[:, 2 * w : 3 * w] + s[:, 3 * w :]
        great_im = c[:, 3 * w :] - s[:, 2 * w : 3 * w]
        prod[rows, :w] = (less_re * great_re + less_im * great_im).astype(jnp.bfloat16)
        prod[rows, w:] = (less_im * great_re - less_re * great_im).astype(jnp.bfloat16)

    @pl.loop(0, count // tile)
    def _(k):
        rows = pl.ds(pl.multiple_of(k * tile, tile), tile)
        c = jnp.dot(cosine[rows, :], prod[...], preferred_element_type=jnp.float32)
        s = jnp.dot(sine[rows, :], prod[...], preferred_element_type=jnp.float32)
        polar_re = weight * (c[:, w:] + s[:, :w])
        polar_im = -weight * (c[:, :w] - s[:, w:])
        square = polar_re * polar_re + polar_im * polar_im
        total[...] += jnp.sum(square.reshape(tile // 8, 8, w), axis=0)
        sent[rows, :w] = polar_re.astype(jnp.bfloat16)
        sent[rows, w:] = polar_im.astype(jnp.bfloat16)


def correlate(columns, cosine, sine):
    count, width = columns.shape
    steps = width // (4 * LANES)
    table = pl.BlockSpec((count, count), lambda t: (0, 0))
    return pl.pallas_call(
        functools.partial(correlate_kernel, min(512, count), float(count) ** (-1.5)),
        grid=(steps,),
        out_shape=(
            jax.ShapeDtypeStruct((count, width // 2), jnp.bfloat16),
            jax.ShapeDtypeStruct((8, LANES), jnp.float32),
        ),
        in_specs=[table, table, pl.BlockSpec((count, 4 * LANES), lambda t: (0, t))],
        out_specs=(
            pl.BlockSpec((count, 2 * LANES), lambda t: (0, t)),
            pl.BlockSpec((8, LANES), lambda t: (0, 0)),
        ),
        scratch_shapes=[pltpu.VMEM((count, 2 * LANES), jnp.bfloat16)],
        compiler_params=pltpu.CompilerParams(vmem_limit_bytes=50 * 1024 * 1024),
        cost_estimate=pl.CostEstimate(
            flops=6 * count * count * width,
            bytes_accessed=3 * count * width,
            transcendentals=0,
        ),
        name="correlate",
    )(cosine, sine, columns)


def exchange(values):
    return lax.all_to_all(values, "ea", split_axis=0, concat_axis=0, tiled=True)


def solution(mesh):
    peers = mesh.shape["ea"]
    everyone = peers * mesh.shape["sa"]

    def body(lesser, greater):
        shape = lesser.shape
        count = shape[1] * peers
        entries = lesser.size // 2 * everyone
        chunks = [
            (block, half) for block in range(shape[2]) for half in range(shape[4] // LANES)
        ]
        totals = []
        returned = []
        arrived = []

        def send(index):
            after = [totals[index - 2]] if index >= 2 else []
            values = pack(lesser, greater, *chunks[index], peers, after)
            arrived.append(exchange(values))

        send(0)
        cosine, sine = lax.optimization_barrier(energy_tables(count))
        for index in range(len(chunks)):
            if index + 1 < len(chunks):
                send(index + 1)
            columns = arrived[index]
            sent, total = correlate(columns.reshape(count, -1), cosine, sine)
            totals.append(total)
            returned.append(exchange(sent.reshape(peers, shape[1], -1)))
        polar = None
        for (block, half), piece in zip(chunks, returned):
            polar = unpack(piece, polar, block, half, shape)
        total = jnp.sum(sum(totals))
        parts = lax.all_to_all(
            jnp.broadcast_to(total, (everyone, LANES)),
            ("ea", "sa"),
            split_axis=0,
            concat_axis=0,
            tiled=True,
        )
        norm_total = jnp.sum(parts[:, 0])
        pol_norm = jnp.sqrt(norm_total / entries + 1e-06).reshape(1)
        return (polar, pol_norm)

    return jax.shard_map(
        body,
        mesh=mesh,
        in_specs=(P(None, "ea", None, "sa", None), P(None, "ea", None, "sa", None)),
        out_specs=(P(None, "ea", None, "sa", None), P()),
        check_vma=False,
    )
```

time: 2320 us -> 1190 us (0.51)
  local copies, waits for them, and re-layouts: 551 us -> 1.84 us
  blocking collectives: 742 us -> 296 us
  Pallas kernels: 0 us -> 262 us
  other arithmetic: 273 us -> 18.8 us
  matrix products: 141 us -> 0 us
    psum x1 -> x0, blocking collectives: 742 us -> none  [body(): norm_total = lax.psum(total, ('ea', 'sa'))]
    all_to_all x0 -> x3, blocking collectives: none -> 296 us  [the longest x2 285 us: exchange(): return lax.all_to_all(values, 'ea', split_axis=0, concat_axis=0, tiled=True)]
    unnamed x10 -> x8, local copies, waits for them, and re-layouts: 290 us -> 1.19 us
    pallas_call x0 -> x12, Pallas kernels: none -> 262 us  [the longest x4 138 us: correlate(): pl.pallas_call(functools.partial(correlate_kernel, min(512, count), float...]
    dot_general x4 -> x0, matrix products: 141 us -> none  [the longest x2 71.1 us: spectra(): jnp.dot(cosine, stacked, preferred_element_type=jnp.float32)]
    all_to_all x1 -> x0, other arithmetic: 98.8 us -> none  [body(): lax.all_to_all(polar_local, 'ea', split_axis=1, concat_axis=4, tiled=True)]
    all_to_all x4 -> x0, local copies, waits for them, and re-layouts: 82.1 us -> none  [the longest x2 57.5 us: body(): lax.all_to_all(polar_local, 'ea', split_axis=1, concat_axis=4, tiled=True)]
    slice x6 -> x0, local copies, waits for them, and re-layouts: 74.8 us -> none  [the longest x2 22.5 us: both_spectra(): less_pairs[1].reshape(energies, width)]
  transfers between devices with their start and end apart: 3 -> 6, of which waited for: 2 -> 6; matrix products, arithmetic and copies ran while one was open for 6% -> 2% of each run, Pallas kernels for 0% -> 20%
where the time goes in v1:
time: 1190 us; the launch traced here: 1180 us
  waiting for transfers between devices  571 us (48%)
  blocking collectives  296 us (25%)
  Pallas kernels  262 us (22%)
  starting transfers between devices  31.6 us (3%)
  other arithmetic  18.8 us (2%)
    all_to_all x6, waiting for transfers between devices, exchange(): return lax.all_to_all(values, 'ea', split_axis=0, concat_axis=0, tiled=True)  571 us
    all_to_all x2, blocking collectives, exchange(): return lax.all_to_all(values, 'ea', split_axis=0, concat_axis=0, tiled=True)  285 us
    pallas_call x4, Pallas kernels, correlate(): pl.pallas_call(functools.partial(correlate_kernel, min(512, count), float...  138 us
    pallas_call x4, Pallas kernels, pack(): pl.pallas_call(functools.partial(pack_kernel, peers, per), grid=(energies...  83.1 us
    pallas_call x4, Pallas kernels, unpack(): pl.pallas_call(functools.partial(unpack_kernel, peers, per), grid=(energi...  41.2 us
    all_to_all x6, starting transfers between devices, exchange(): return lax.all_to_all(values, 'ea', split_axis=0, concat_axis=0, tiled=True)  31.6 us
  transfers between devices with their start and end apart: 6, of which 6 were waited for; matrix products, arithmetic and copies ran while one was open for 2% of the time, Pallas kernels for 20%

profile of v1, /device:TPU:0, one launch (start us, length us, event | category | flops | bytes accessed | tf_op | source)
XLA Modules:
  0.0 1184.1 jit_solution(18302044099346704261)
XLA Ops:
  0.6 20.8 %pack.4 = bf16[8,128,4096]{2,1,0:T(8,128)(2,1)} custom-call(bf16[2,128,2,64,256]{4,3,2,1,0:T(8,128)(2,1)} %less_ref.7, bf16[2,128,2,64,256]{4,3,2,1,0:T(8,128)(2,1)} %great_ref.7), custom_call_target="tpu_custom_call" | custom-call | bytes 16777216 | tf_op jit(solution)/shard_map/pack/pallas_call | solution.py:42
  21.4 7.3 all-to-all-start
  28.7 20.8 %pack.6 = bf16[8,128,4096]{2,1,0:T(8,128)(2,1)} custom-call(bf16[2,128,2,64,256]{4,3,2,1,0:T(8,128)(2,1)} %less_ref.7, bf16[2,128,2,64,256]{4,3,2,1,0:T(8,128)(2,1)} %great_ref.7), custom_call_target="tpu_custom_call" | custom-call | bytes 16777216 | tf_op jit(solution)/shard_map/pack/pallas_call | solution.py:42
  49.5 162.4 %all-to-all-done = bf16[8,128,4096]{2,1,0:T(8,128)(2,1)} async-done(((bf16[8,128,4096]{2,1,0:T(8,128)(2,1)}), bf16[8,128,4096]{2,1,0:T(8,128)(2,1)}, u32[]{:S(2)}, u32[]{:S(2)}) %all-to-all-start) | async-done | bytes 8388640 | tf_op jit(solution)/shard_map/all_to_all | solution.py:152
  217.0 17.6 %sine_convert_fusion = (bf16[1024,1024]{1,0:T(8,128)(2,1)}, bf16[1024,1024]{1,0:T(8,128)(2,1)S(1)}) fusion(), kind=kLoop, calls=%fused_computation.6 | loop fusion | flops 16777216 | bytes 4194304 | tf_op jit(solution)/shard_map/convert_element_type | solution.py:18
  234.6 34.5 %correlate.4 = (bf16[1024,2048]{1,0:T(8,128)(2,1)}, f32[8,128]{1,0:T(8,128)S(1)}) custom-call(bf16[1024,1024]{1,0:T(8,128)(2,1)S(1)} %get-tuple-element.12.cosine, bf16[1024,1024]{1,0:T(8,128)(2,1)} %get-tuple-element.13.sine, bf16[1024,4096]{1,0:T(8,128)(2,1)} %bitcast.columns), custom_call_target="tpu_custom_call" | custom-call | flops 25769803776 | bytes 12582912 | tf_op jit(solution)/shard_map/correlate/pallas_call | solution.py:128
  269.7 129.3 %all-to-all-done.3 = bf16[8,128,4096]{2,1,0:T(8,128)(2,1)} async-done(((bf16[8,128,4096]{2,1,0:T(8,128)(2,1)}), bf16[8,128,4096]{2,1,0:T(8,128)(2,1)}, u32[]{:S(2)}, u32[]{:S(2)}) %all-to-all-start.3) | async-done | bytes 8388640 | tf_op jit(solution)/shard_map/all_to_all | solution.py:152
  403.7 20.8 %pack.5 = bf16[8,128,4096]{2,1,0:T(8,128)(2,1)} custom-call(bf16[2,128,2,64,256]{4,3,2,1,0:T(8,128)(2,1)} %less_ref.7, bf16[2,128,2,64,256]{4,3,2,1,0:T(8,128)(2,1)} %great_ref.7, f32[8,128]{1,0:T(8,128)} %copy-done), custom_call_target="tpu_custom_call" | custom-call | bytes 16777216 | tf_op jit(solution)/shard_map/pack/pallas_call | solution.py:42
  424.5 71.8 %all-to-all-done.6.source = bf16[8,128,2048]{2,1,0:T(8,128)(2,1)} async-done(((bf16[8,128,2048]{2,1,0:T(8,128)(2,1)}), bf16[8,128,2048]{2,1,0:T(8,128)(2,1)}, u32[]{:S(2)}, u32[]{:S(2)}) %all-to-all-start.6) | async-done | bytes 4194336 | tf_op jit(solution)/shard_map/all_to_all | solution.py:152
  496.3 5.3 all-to-all-start.1
  501.6 34.5 %correlate.6 = (bf16[1024,2048]{1,0:T(8,128)(2,1)}, f32[8,128]{1,0:T(8,128)S(1)}) custom-call(bf16[1024,1024]{1,0:T(8,128)(2,1)S(1)} %get-tuple-element.12.cosine, bf16[1024,1024]{1,0:T(8,128)(2,1)} %get-tuple-element.13.sine, bf16[1024,4096]{1,0:T(8,128)(2,1)} %bitcast.3.columns), custom_call_target="tpu_custom_call" | custom-call | flops 25769803776 | bytes 12582912 | tf_op jit(solution)/shard_map/correlate/pallas_call | solution.py:128
  536.7 20.8 %pack.7 = bf16[8,128,4096]{2,1,0:T(8,128)(2,1)} custom-call(bf16[2,128,2,64,256]{4,3,2,1,0:T(8,128)(2,1)} %less_ref.7, bf16[2,128,2,64,256]{4,3,2,1,0:T(8,128)(2,1)} %great_ref.7, f32[8,128]{1,0:T(8,128)} %copy-done.2), custom_call_target="tpu_custom_call" | custom-call | bytes 16777216 | tf_op jit(solution)/shard_map/pack/pallas_call | solution.py:42
  557.4 125.9 %all-to-all-done.1 = bf16[8,128,4096]{2,1,0:T(8,128)(2,1)} async-done(((bf16[8,128,4096]{2,1,0:T(8,128)(2,1)}), bf16[8,128,4096]{2,1,0:T(8,128)(2,1)}, u32[]{:S(2)}, u32[]{:S(2)}) %all-to-all-start.1) | async-done | bytes 8388640 | tf_op jit(solution)/shard_map/all_to_all | solution.py:152
  683.4 187.4 %all_to_all.49 = bf16[8,128,4096]{2,1,0:T(8,128)(2,1)} all-to-all(bf16[8,128,4096]{2,1,0:T(8,128)(2,1)} %pack.7), channel_id=1, replica_groups=mesh['ea'=8,'sa'=4] {'ea'}, dimensions={0} | all-to-all | bytes 16777216 | tf_op jit(solution)/shard_map/all_to_all | solution.py:152
  875.4 34.5 %correlate.5 = (bf16[1024,2048]{1,0:T(8,128)(2,1)}, f32[8,128]{1,0:T(8,128)S(1)}) custom-call(bf16[1024,1024]{1,0:T(8,128)(2,1)S(1)} %get-tuple-element.12.cosine, bf16[1024,1024]{1,0:T(8,128)(2,1)} %get-tuple-element.13.sine, bf16[1024,4096]{1,0:T(8,128)(2,1)} %bitcast.1.columns), custom_call_target="tpu_custom_call" | custom-call | flops 25769803776 | bytes 12582912 | tf_op jit(solution)/shard_map/correlate/pallas_call | solution.py:128
  909.9 34.4 %correlate.7 = (bf16[1024,2048]{1,0:T(8,128)(2,1)}, f32[8,128]{1,0:T(8,128)S(1)}) custom-call(bf16[1024,1024]{1,0:T(8,128)(2,1)S(1)} %get-tuple-element.12.cosine, bf16[1024,1024]{1,0:T(8,128)(2,1)} %get-tuple-element.13.sine, bf16[1024,4096]{1,0:T(8,128)(2,1)} %bitcast.10), custom_call_target="tpu_custom_call" | custom-call | flops 25769803776 | bytes 12582912 | tf_op jit(solution)/shard_map/correlate/pallas_call | solution.py:128
  944.9 21.6 %all-to-all-done.7.source = bf16[8,128,2048]{2,1,0:T(8,128)(2,1)} async-done(((bf16[8,128,2048]{2,1,0:T(8,128)(2,1)}), bf16[8,128,2048]{2,1,0:T(8,128)(2,1)}, u32[]{:S(2)}, u32[]{:S(2)}) %all-to-all-start.7) | async-done | bytes 4194336 | tf_op jit(solution)/shard_map/all_to_all | solution.py:152
  967.2 10.6 all_to_all.50
  977.8 97.9 %all_to_all.51.source = bf16[8,128,2048]{2,1,0:T(8,128)(2,1)} all-to-all(bf16[8,128,2048]{2,1,0:T(8,128)(2,1)} %bitcast.13), channel_id=1, replica_groups=mesh['ea'=8,'sa'=4] {'ea'}, dimensions={0} | all-to-all | bytes 8388608 | tf_op jit(solution)/shard_map/all_to_all | solution.py:152
  1080.6 10.3 unpack.4.rest_0_
  1090.9 10.3 unpack.5.rest_0_
  1102.5 10.3 unpack.6.rest_0_
  1112.8 59.9 %all-to-all-done.2.source = bf16[8,128,2048]{2,1,0:T(8,128)(2,1)} async-done(((bf16[8,128,2048]{2,1,0:T(8,128)(2,1)}), bf16[8,128,2048]{2,1,0:T(8,128)(2,1)}, u32[]{:S(2)}, u32[]{:S(2)}) %all-to-all-start.2) | async-done | bytes 4194336 | tf_op jit(solution)/shard_map/all_to_all | solution.py:152
  1172.6 10.3 unpack.7
  (15 shorter events, 22.1 us)
Async XLA Ops:
  21.4 190.5 %all-to-all-start = ((bf16[8,128,4096]{2,1,0:T(8,128)(2,1)}), bf16[8,128,4096]{2,1,0:T(8,128)(2,1)}, u32[]{:S(2)}, u32[]{:S(2)}) async-start(bf16[8,128,4096]{2,1,0:T(8,128)(2,1)} %pack.4), calls=%async_computation | async-start | bytes 16777216 | tf_op jit(solution)/shard_map/all_to_all | solution.py:152
  211.9 187.2 %all-to-all-start.3 = ((bf16[8,128,4096]{2,1,0:T(8,128)(2,1)}), bf16[8,128,4096]{2,1,0:T(8,128)(2,1)}, u32[]{:S(2)}, u32[]{:S(2)}) async-start(bf16[8,128,4096]{2,1,0:T(8,128)(2,1)} %pack.6), calls=%async_computation.3 | async-start | bytes 16777216 | tf_op jit(solution)/shard_map/all_to_all | solution.py:152
  269.1 0.6 copy-start
  399.1 97.2 %all-to-all-start.6 = ((bf16[8,128,2048]{2,1,0:T(8,128)(2,1)}), bf16[8,128,2048]{2,1,0:T(8,128)(2,1)}, u32[]{:S(2)}, u32[]{:S(2)}) async-start(bf16[8,128,2048]{2,1,0:T(8,128)(2,1)} %bitcast.14), calls=%async_computation.6 | async-start | bytes 8388608 | tf_op jit(solution)/shard_map/all_to_all | solution.py:152
  496.3 187.1 %all-to-all-start.1 = ((bf16[8,128,4096]{2,1,0:T(8,128)(2,1)}), bf16[8,128,4096]{2,1,0:T(8,128)(2,1)}, u32[]{:S(2)}, u32[]{:S(2)}) async-start(bf16[8,128,4096]{2,1,0:T(8,128)(2,1)} %pack.5), calls=%async_computation.1 | async-start | bytes 16777216 | tf_op jit(solution)/shard_map/all_to_all | solution.py:152
  536.1 0.6 copy-start.2
  870.8 95.7 %all-to-all-start.7 = ((bf16[8,128,2048]{2,1,0:T(8,128)(2,1)}), bf16[8,128,2048]{2,1,0:T(8,128)(2,1)}, u32[]{:S(2)}, u32[]{:S(2)}) async-start(bf16[8,128,2048]{2,1,0:T(8,128)(2,1)} %bitcast.12), calls=%async_computation.7 | async-start | bytes 8388608 | tf_op jit(solution)/shard_map/all_to_all | solution.py:152
  909.8 34.5 %copy-start.1 = (f32[8,128]{1,0:T(8,128)S(1)}, f32[8,128]{1,0:T(8,128)}, u32[]{:S(2)}) copy-start(f32[8,128]{1,0:T(8,128)} %copy-done) | copy-start | bytes 12292
  909.8 34.5 %copy-start.3 = (f32[8,128]{1,0:T(8,128)S(1)}, f32[8,128]{1,0:T(8,128)}, u32[]{:S(2)}) copy-start(f32[8,128]{1,0:T(8,128)} %copy-done.2) | copy-start | bytes 12292
  1075.8 96.9 %all-to-all-start.2 = ((bf16[8,128,2048]{2,1,0:T(8,128)(2,1)}), bf16[8,128,2048]{2,1,0:T(8,128)(2,1)}, u32[]{:S(2)}, u32[]{:S(2)}) async-start(bf16[8,128,2048]{2,1,0:T(8,128)(2,1)} %bitcast.11), calls=%async_computation.2 | async-start | bytes 8388608 | tf_op jit(solution)/shard_map/all_to_all | solution.py:152
